TPU v7x, 512 devices: a whole 4x8x8 slice. The times are simulated.
512 devices in a mesh: rep: 8 (over z), fsdp: 64 (over y, x, core).
Axes of the slice: x: 4, y: 8, z: 8, core: 2. Of those that a mesh axis runs over, the one named last changes fastest.
Arguments:
- accumulated: bfloat16 [8, 4096, 14336], P('rep', 'fsdp'), may hold values from -16 to 16
- q_start: bfloat16 [32, 14336], P(None, 'fsdp'), may hold values from -6 to 6
Outputs:
- residual_buffer: bfloat16 [8, 4096, 14336], P('rep', 'fsdp')
- basis_f32: float32 [4096, 32], P('fsdp')
- q_factor: float32 [32, 14336], P(None, 'fsdp')
All inputs are finite; a program needn't handle non-finite values.
Results may differ from a plain program's by a relative error of at most 0.0039.
Values may be sent and summed in bfloat16 or wider, within the bound.
A program may use at most 64 MiB of HBM per device.

v0:
```python
import jax
import jax.numpy as jnp
from jax import lax
from jax.sharding import PartitionSpec as P

ITERS = 2


def from_everyone(x, axis):
    peers = lax.axis_size(axis)
    return lax.all_to_all(jnp.broadcast_to(x[None], (peers, *x.shape)), axis, 0, 0, tiled=True)


def over_copies(x, axis):
    return from_everyone(x, axis).sum(axis=0)


def in_order(blocks, dim):
    blocks = jnp.moveaxis(blocks, 0, dim)
    shape = blocks.shape
    return blocks.reshape(*shape[:dim], shape[dim] * shape[dim + 1], *shape[dim + 2 :])


def collect(x, axis, dim):
    blocks = from_everyone(x, axis)
    return in_order(blocks, dim)


def in_blocks(x, dim, peers):
    before, after = (x.shape[:dim], x.shape[dim + 1 :])
    return jnp.moveaxis(x.reshape(*before, peers, -1, *after), dim, 0)


def summed_on_arrival(x, axis, dim):
    blocks = in_blocks(x, dim, lax.axis_size(axis))
    arrived = lax.all_to_all(blocks, axis, split_axis=0, concat_axis=0, tiled=True)
    return arrived.sum(axis=0)


def orthonormal(p_sum):
    partial_gram = jnp.dot(p_sum.T, p_sum, precision=lax.Precision.HIGHEST)
    gram_matrix = over_copies(partial_gram, "fsdp")
    factor = jnp.linalg.cholesky(gram_matrix)
    return lax.linalg.triangular_solve(factor, p_sum, left_side=False, lower=True, transpose_a=True)


def on_device(accumulated, q_start):
    own_rows = accumulated[0]
    replicas = lax.axis_size("rep")
    right_factor = q_start
    for iteration in range(ITERS):
        if iteration == 0:
            term = lax.dot_general(
                own_rows,
                collect(q_start, "fsdp", 1),
                (((1,), (1,)), ((), ())),
                preferred_element_type=jnp.float32,
            )
            p_local = term
        else:
            p_local = lax.dot_general(
                own_rows, right_factor, (((1,), (1,)), ((), ())), preferred_element_type=jnp.float32
            )
        p_sum = over_copies(p_local, "rep")
        basis_f32 = orthonormal(p_sum)
        basis_bf16 = basis_f32.astype(jnp.bfloat16)
        q_term = lax.dot_general(
            basis_bf16, own_rows, (((0,), (0,)), ((), ())), preferred_element_type=jnp.float32
        )
        q_group = summed_on_arrival(q_term, "fsdp", 1)
        q_owned = over_copies(q_group, "rep") / replicas
        right_factor = collect(q_owned.astype(jnp.bfloat16), "fsdp", 1)
    approx = lax.dot_general(
        basis_bf16, right_factor, (((1,), (0,)), ((), ())), preferred_element_type=jnp.float32
    )
    residual_buffer = (own_rows.astype(jnp.float32) - approx).astype(jnp.bfloat16)[None]
    return (residual_buffer, basis_f32, q_owned)


def solution(mesh):
    in_specs = (P("rep", "fsdp", None), P(None, "fsdp"))
    out_specs = (P("rep", "fsdp", None), P("fsdp", None), P(None, "fsdp"))
    return jax.shard_map(
        on_device, mesh=mesh, in_specs=in_specs, out_specs=out_specs, check_vma=False
    )
```

profile of v0, /device:TPU:1, one launch (start us, length us, event | category | flops | bytes accessed | tf_op | source)
XLA Modules:
  0.0 366.2 jit_solution(14121992070788439460)
XLA Ops:
  0.6 0.8 broadcast_in_dim.21
  1.5 39.6 %all_to_all.55 = bf16[64,32,224]{2,1,0:T(8,128)(2,1)S(1)} all-to-all(bf16[64,32,224]{2,1,0:T(8,128)(2,1)S(1)} %broadcast_in_dim.21), channel_id=1, replica_groups=mesh['rep'=8,'fsdp'=64] {'fsdp'}, dimensions={0} | all-to-all | bytes 1835008 | tf_op jit(solution)/shard_map/all_to_all | solution.py:11
  41.6 2.8 reshape.45
  44.4 1.8 fusion.8
  46.4 17.1 %all_to_all.56 = f32[8,1,2048]{2,1,0:T(1,128)S(1)} all-to-all(f32[8,1,2048]{2,1,0:T(1,128)S(1)} %reshape.56), channel_id=1, replica_groups=mesh['rep'=8,'fsdp'=64] {'rep'}, dimensions={0} | all-to-all | bytes 131072 | tf_op jit(solution)/shard_map/all_to_all | solution.py:11
  65.1 1.2 reshape.58
  66.3 7.7 %all-to-all-start.2 = ((f32[64,1,1024]{2,1,0:T(1,128)}), f32[64,1,1024]{2,1,0:T(1,128)S(1)}, u32[]{:S(2)}, u32[]{:S(2)}) async-start(f32[64,1,1024]{2,1,0:T(1,128)} %reshape.58), calls=%async_computation.2 | async-start | bytes 524288 | tf_op jit(solution)/shard_map/all_to_all | solution.py:11
  74.0 4.0 %dot_general.30 = bf16[64,224,64]{1,0,2:T(8,128)(2,1)} reshape(bf16[14336,64]{0,1:T(8,128)(2,1)S(1)} %bitcast.72) | data formatting | bytes 3670016 | tf_op jit(solution)/shard_map/dot_general | solution.py:67
  78.0 9.1 %all-to-all-done.2 = f32[64,1,1024]{2,1,0:T(1,128)S(1)} async-done(((f32[64,1,1024]{2,1,0:T(1,128)}), f32[64,1,1024]{2,1,0:T(1,128)S(1)}, u32[]{:S(2)}, u32[]{:S(2)}) %all-to-all-start.2) | async-done | bytes 262176 | tf_op jit(solution)/shard_map/all_to_all | solution.py:11
  87.1 1.3 reduce.5
  88.9 2.9 cholesky.44
  93.1 2.4 custom-call.6
  95.8 3.2 fusion.10
  99.0 54.4 %all_to_all.57 = f32[64,32,224]{2,1,0:T(8,128)} all-to-all(f32[64,32,224]{2,1,0:T(8,128)S(1)} %fusion.10), channel_id=1, replica_groups=mesh['rep'=8,'fsdp'=64] {'fsdp'}, dimensions={0} | all-to-all | bytes 3670016 | tf_op jit(solution)/shard_map/all_to_all | solution.py:36
  153.4 1.8 reduce_sum.74
  155.2 11.7 %all_to_all.58 = f32[8,32,224]{2,1,0:T(8,128)S(1)} all-to-all(f32[8,32,224]{2,1,0:T(8,128)S(1)} %broadcast_in_dim.24), channel_id=1, replica_groups=mesh['rep'=8,'fsdp'=64] {'rep'}, dimensions={0} | all-to-all | bytes 458752 | tf_op jit(solution)/shard_map/all_to_all | solution.py:11
  167.0 37.7 %all_to_all.59 = bf16[64,32,224]{2,1,0:T(8,128)(2,1)S(1)} all-to-all(bf16[64,32,224]{2,1,0:T(8,128)(2,1)S(1)} %broadcast_in_dim.25), channel_id=1, replica_groups=mesh['rep'=8,'fsdp'=64] {'fsdp'}, dimensions={0} | all-to-all | bytes 1835008 | tf_op jit(solution)/shard_map/all_to_all | solution.py:11
  205.3 2.8 reshape.46
  208.1 1.8 fusion.16
  210.0 9.6 %all_to_all.60 = f32[8,1,2048]{2,1,0:T(1,128)S(1)} all-to-all(f32[8,1,2048]{2,1,0:T(1,128)S(1)} %reshape.60), channel_id=1, replica_groups=mesh['rep'=8,'fsdp'=64] {'rep'}, dimensions={0} | all-to-all | bytes 131072 | tf_op jit(solution)/shard_map/all_to_all | solution.py:11
  219.6 0.8 reduce.6
  221.3 20.3 %all_to_all.61 = f32[64,1,1024]{2,1,0:T(1,128)S(1)} all-to-all(f32[64,1,1024]{2,1,0:T(1,128)S(1)} %reshape.62), channel_id=1, replica_groups=mesh['rep'=8,'fsdp'=64] {'fsdp'}, dimensions={0} | all-to-all | bytes 524288 | tf_op jit(solution)/shard_map/all_to_all | solution.py:11
  241.5 1.3 reduce.7
  243.3 2.9 cholesky.55
  247.6 2.4 custom-call.7
  250.3 3.2 fusion.13
  253.5 54.4 %all_to_all.62 = f32[64,32,224]{2,1,0:T(8,128)} all-to-all(f32[64,32,224]{2,1,0:T(8,128)S(1)} %fusion.13), channel_id=1, replica_groups=mesh['rep'=8,'fsdp'=64] {'fsdp'}, dimensions={0} | all-to-all | bytes 3670016 | tf_op jit(solution)/shard_map/all_to_all | solution.py:36
  307.9 1.8 reduce_sum.78
  309.7 11.7 %all_to_all.63 = f32[8,32,224]{2,1,0:T(8,128)S(1)} all-to-all(f32[8,32,224]{2,1,0:T(8,128)S(1)} %broadcast_in_dim.28), channel_id=1, replica_groups=mesh['rep'=8,'fsdp'=64] {'rep'}, dimensions={0} | all-to-all | bytes 458752 | tf_op jit(solution)/shard_map/all_to_all | solution.py:11
  322.1 37.7 %all_to_all.64 = bf16[64,32,224]{2,1,0:T(8,128)(2,1)S(1)} all-to-all(bf16[64,32,224]{2,1,0:T(8,128)(2,1)S(1)} %broadcast_in_dim.29), channel_id=1, replica_groups=mesh['rep'=8,'fsdp'=64] {'fsdp'}, dimensions={0} | all-to-all | bytes 1835008 | tf_op jit(solution)/shard_map/all_to_all | solution.py:11
  360.4 2.8 reshape.47
  363.2 3.1 fusion.1
  (46 shorter events, 9.7 us)
Async XLA Ops:
  41.0 3.4 copy-start
  66.3 20.8 %all-to-all-start.2 = ((f32[64,1,1024]{2,1,0:T(1,128)}), f32[64,1,1024]{2,1,0:T(1,128)S(1)}, u32[]{:S(2)}, u32[]{:S(2)}) async-start(f32[64,1,1024]{2,1,0:T(1,128)} %reshape.58), calls=%async_computation.2 | async-start | bytes 524288 | tf_op jit(solution)/shard_map/all_to_all | solution.py:11
  250.3 112.9 %copy-start.1 = (f32[64,32]{0,1:T(8,128)}, f32[64,32]{0,1:T(8,128)S(1)}, u32[]{:S(2)}) copy-start(f32[64,32]{0,1:T(8,128)S(1)} %convolution_bitcast_fusion) | copy-start | bytes 24580
where the time goes:
time: 367 us; the launch traced here: 366 us
  blocking collectives  294 us (80%)
  other arithmetic  21.9 us (6%)
  local copies, waits for them, and re-layouts  18.8 us (5%)
  matrix products  13.8 us (4%)
  waiting for transfers between devices  9.09 us (2%)
  starting transfers between devices  7.7 us (2%)
    all_to_all x8, blocking collectives, from_everyone(): lax.all_to_all(jnp.broadcast_to(x[None], (peers, *x.shape)), axis, 0, 0,...  185 us
    all_to_all x2, blocking collectives, summed_on_arrival(): lax.all_to_all(blocks, axis, split_axis=0, concat_axis=0, tiled=True)  109 us
    all_to_all x1, waiting for transfers between devices, from_everyone(): lax.all_to_all(jnp.broadcast_to(x[None], (peers, *x.shape)), axis, 0, 0,...  9.09 us
    reshape x3, local copies, waits for them, and re-layouts, in_order(): blocks.reshape(*shape[:dim], shape[dim] * shape[dim + 1], *shape[dim + 2:])  8.33 us
    all_to_all x1, starting transfers between devices, from_everyone(): lax.all_to_all(jnp.broadcast_to(x[None], (peers, *x.shape)), axis, 0, 0,...  7.7 us
  transfers between devices with their start and end apart: 1, of which 1 were waited for; matrix products, arithmetic and copies ran while one was open for 1% of the time, Pallas kernels for 0%

commit v1 on v0

v1 whole, which is shorter than its diff:
```python
import functools

import jax
import jax.numpy as jnp
from jax import lax
from jax.experimental import pallas as pl
from jax.experimental.pallas import tpu as pltpu
from jax.sharding import PartitionSpec as P

ITERS = 2
NX = 4
NC = 2
WIDE = 256
MESH = pl.DeviceIdType.MESH
HIGHEST = lax.Precision.HIGHEST
NT = (((1,), (1,)), ((), ()))


def near_first(n):
    return sorted(range(1, n), key=lambda d: (min(d, n - d), d))


def kernel(
    nz,
    ny,
    a_hbm,
    q_ref,
    flat_ref,
    basis_ref,
    q_out,
    a_flat,
    a_pad,
    right,
    left,
    own_left,
    gram_c,
    gram_x,
    gram_y,
    w,
    w_c,
    w_x,
    w_xs,
    w_y,
    w_z,
    a_sem,
    ag_s,
    ag_r,
    p_s,
    p_r,
    g_s,
    g_r,
    w_s,
    w_r,
):
    rank, cols = q_ref.shape
    rows = a_flat.shape[0]
    z = lax.axis_index("rep")
    f = lax.axis_index("fsdp")
    c = lax.rem(f, NC)
    x = lax.rem(f // NC, NX)
    y = f // (NC * NX)
    other = 1 - c
    dxs, dys, dzs = near_first(NX), near_first(ny), near_first(nz)

    def at(yy, xx, cc):
        return (yy * NX + xx) * NC + cc

    def to(src, dst, send, recv, device):
        return pltpu.make_async_remote_copy(
            src_ref=src,
            dst_ref=dst,
            send_sem=send,
            recv_sem=recv,
            device_id=device,
            device_id_type=MESH,
        )

    x_of = [lax.rem(x + d, NX) for d in dxs]
    y_of = [lax.rem(y + d, ny) for d in dys]
    z_of = [lax.rem(z + d, nz) for d in dzs]
    x_from = [lax.rem(x + NX - d, NX) for d in dxs]
    x_peers = [(z, at(y, xx, c)) for xx in x_of]
    y_peers = [(z, at(yy, x, c)) for yy in y_of]
    z_peers = [(zz, f) for zz in z_of]
    mate = (z, at(y, x, other))

    load = pltpu.make_async_copy(a_hbm.at[0], a_flat, a_sem)
    load.start()
    barrier = pltpu.get_barrier_semaphore()
    everyone = [mate] + x_peers + y_peers + z_peers
    for peer in everyone:
        pl.semaphore_signal(barrier, inc=1, device_id=peer, device_id_type=MESH)
    right[0, c, x, y] = jnp.zeros((rank, WIDE), jnp.bfloat16)
    right[0, c, x, y, :, :cols] = q_ref[...]
    pl.semaphore_wait(barrier, len(everyone))

    def start_gather(v):
        own = right.at[v, c, x, y]
        copies = []
        for i, peer in enumerate(y_peers):
            copy = to(own, own, ag_s.at[v, i], ag_r.at[v, i], peer)
            copy.start()
            copies.append(copy)
        return copies

    def chunk(v, cc, xx):
        r = right[v, cc, xx]
        r = jnp.concatenate([r[j] for j in range(ny)], axis=1)
        return lax.dot_general(r, a_pad[cc * NX + xx], NT, preferred_element_type=jnp.float32)

    def finish_gather(v, copies, multiply=True):
        base = len(copies)
        for copy in copies:
            copy.wait_recv()
        sent, crossed, arriving = list(copies), [], []
        slab = right.at[v, c, x]
        for i, peer in enumerate(x_peers):
            copy = to(slab, slab, ag_s.at[v, base + i], ag_r.at[v, base + i], peer)
            copy.start()
            arriving.append(copy)
        base += len(arriving)

        def cross(i, xx):
            part = right.at[v, c, xx]
            copy = to(part, part, ag_s.at[v, base + i], ag_r.at[v, base + i], mate)
            copy.start()
            crossed.append(copy)

        cross(0, x)
        total = chunk(v, c, x) if multiply else None
        for i, copy in enumerate(arriving):
            copy.wait_recv()
            cross(i + 1, x_from[i])
            if multiply:
                total += chunk(v, c, x_from[i])
        for i, copy in enumerate(crossed):
            copy.wait_recv()
            if multiply:
                total += chunk(v, other, x if i == 0 else x_from[i - 1])
        for copy in sent + arriving + crossed:
            copy.wait_send()
        return total

    def exchange(buffer, slot, peers, send, recv):
        copies = []
        for i, peer in enumerate(peers):
            copy = to(buffer.at[slot], buffer.at[slot], send.at[i], recv.at[i], peer)
            copy.start()
            copies.append(copy)
        return copies

    def summed(buffer, n):
        total = buffer[0]
        for i in range(1, n):
            total += buffer[i]
        return total

    copies = start_gather(0)
    load.wait()
    for g in range(a_flat.shape[1] // (4 * cols)):
        four = a_flat[:, g * 4 * cols : (g + 1) * 4 * cols]
        for j in range(4):
            b = 4 * g + j
            bc, bx, by = b % NC, (b // NC) % NX, b // (NC * NX)
            part = jnp.concatenate(
                [four[:, j * cols : (j + 1) * cols], jnp.zeros((rows, WIDE - cols), jnp.bfloat16)],
                axis=1,
            )
            a_pad[bc * NX + bx, :, by * WIDE : (by + 1) * WIDE] = part

    half = rank // 2
    for it in range(ITERS):
        term = finish_gather(it, copies)
        left[it, z] = jnp.concatenate([term[:half], term[half:]], axis=1)
        sends = exchange(left.at[it], z, z_peers, p_s.at[it], p_r.at[it])
        for copy in sends:
            copy.wait()
        packed = summed(left.at[it], nz)
        pt = jnp.concatenate([packed[:, :rows], packed[:, rows:]], axis=0)

        below = jnp.concatenate([pt, jnp.zeros((128 - rank, rows), jnp.float32)], axis=0)
        gram = lax.dot_general(
            pt, below, NT, precision=HIGHEST, preferred_element_type=jnp.float32
        )
        gp = gram[0:8]
        for k in range(1, rank // 8):
            gp += pltpu.roll(gram[8 * k : 8 * k + 8], rank * k, 1)
        gram_c[it, c] = gp
        g_c = exchange(gram_c.at[it], c, [mate], g_s.at[it, pl.ds(0, 1)], g_r.at[it, pl.ds(0, 1)])

        hi = pt.astype(jnp.bfloat16)
        lo = (pt - hi.astype(jnp.float32)).astype(jnp.bfloat16)
        hl = jnp.concatenate([hi, lo], axis=0)

        def outer(cc, xx):
            both = lax.dot_general(
                hl,
                a_pad[cc * NX + xx],
                (((1,), (0,)), ((), ())),
                preferred_element_type=jnp.float32,
            )
            one = both[:rank] + both[rank:]
            for j in range(ny):
                w[it, cc, xx, j] = one[:, j * WIDE : (j + 1) * WIDE]

        order = x_of + [x]
        crossed = []
        for i, xx in enumerate(order):
            outer(other, xx)
            copy = to(w.at[it, other, xx], w_c.at[it, xx], w_s.at[it, i], w_r.at[it, i], mate)
            copy.start()
            crossed.append(copy)
        for copy in g_c:
            copy.wait()
        gram_x[it, x] = gram_c[it, 0] + gram_c[it, 1]
        g_x = exchange(
            gram_x.at[it], x, x_peers, g_s.at[it, pl.ds(1, NX - 1)], g_r.at[it, pl.ds(1, NX - 1)]
        )
        for xx in order:
            outer(c, xx)
        base = NX
        moved = []
        for i, xx in enumerate(x_of):
            crossed[i].wait_recv()
            w_xs[it, i] = w[it, c, xx] + w_c[it, xx]
            copy = to(
                w_xs.at[it, i], w_x.at[it, i], w_s.at[it, base + i], w_r.at[it, base + i], x_peers[i]
            )
            copy.start()
            moved.append(copy)
        base += len(moved)
        for copy in g_x:
            copy.wait()
        gram_y[it, y] = summed(gram_x.at[it], NX)
        g_y = exchange(
            gram_y.at[it], y, y_peers, g_s.at[it, pl.ds(NX, ny - 1)], g_r.at[it, pl.ds(NX, ny - 1)]
        )
        crossed[-1].wait_recv()
        w[it, c, x] = w[it, c, x] + w_c[it, x]
        for copy in moved:
            copy.wait_recv()
        for j in range(ny):
            w[it, c, x, j] = (w[it, c, x, j] + w_x[it, 0, j]) + summed(
                w_x.at[it, pl.ds(1, NX - 2), j], NX - 2
            )
        spread = []
        for i, yy in enumerate(y_of):
            copy = to(
                w.at[it, c, x, yy], w_y.at[it, i], w_s.at[it, base + i], w_r.at[it, base + i], y_peers[i]
            )
            copy.start()
            spread.append(copy)
        base += len(spread)
        for copy in g_y:
            copy.wait()
        gp = summed(gram_y.at[it], ny)
        lane = lax.broadcasted_iota(jnp.int32, (rank, 128), 1)
        row = lax.broadcasted_iota(jnp.int32, (rank, 128), 0)
        m = jnp.concatenate(
            [pltpu.roll(gp, (rank + 128 - rank * k) % 128, 1) for k in range(rank // 8)], axis=0
        )
        in_gram = (lane >= rank) & (lane < 2 * rank)
        m = jnp.where(in_gram, m, jnp.where(lane == row, 1.0, 0.0))
        scale = jnp.zeros((rank, 128), jnp.float32)
        for k in range(rank):
            pivot = m[k : k + 1, rank + k : rank + k + 1]
            column = m[:, rank + k : rank + k + 1] * (1.0 / pivot)
            scale = jnp.where(row == k, jnp.broadcast_to(lax.rsqrt(pivot), (rank, 128)), scale)
            m = m - jnp.where(row > k, column, 0.0) * m[k : k + 1, :]
        inverse = (m * scale)[:, :rank]
        for copy in spread:
            copy.wait_recv()
        w_z[it, z] = w[it, c, x, y] + summed(w_y.at[it], ny - 1)
        last = exchange(w_z.at[it], z, z_peers, w_s.at[it, pl.ds(base, nz - 1)], w_r.at[it, pl.ds(base, nz - 1)])
        if it == ITERS - 1:
            basis_ref[...] = jnp.dot(
                inverse, pt, precision=HIGHEST, preferred_element_type=jnp.float32
            )
        for copy in last:
            copy.wait_recv()
        q = jnp.dot(
            inverse, summed(w_z.at[it], nz), precision=HIGHEST, preferred_element_type=jnp.float32
        ) / nz
        right[it + 1, c, x, y] = q.astype(jnp.bfloat16)
        copies = start_gather(it + 1)
        if it == ITERS - 1:
            q_out[...] = q[:, :cols]
        for copy in crossed + moved + spread + last:
            copy.wait_send()

    finish_gather(ITERS, copies, multiply=False)
    for g in range(a_flat.shape[1] // (4 * cols)):
        parts = []
        for j in range(4):
            b = 4 * g + j
            bc, bx, by = b % NC, (b // NC) % NX, b // (NC * NX)
            parts.append(right[ITERS, bc, bx, by][:, :cols])
        flat_ref[:, g * 4 * cols : (g + 1) * 4 * cols] = jnp.concatenate(parts, axis=1)


def on_device(nz, nf, accumulated, q_start):
    rank, cols = q_start.shape
    rows = accumulated.shape[1]
    ny = nf // (NX * NC)
    bf, f32 = jnp.bfloat16, jnp.float32
    vmem = pltpu.VMEM
    dma = pltpu.SemaphoreType.DMA
    n_ag = ny - 1 + NX - 1 + NX
    n_g = 1 + NX - 1 + ny - 1
    n_w = NX + NX - 1 + ny - 1 + nz - 1
    flat, basis_t, q_factor = pl.pallas_call(
        functools.partial(kernel, nz, ny),
        out_shape=(
            jax.ShapeDtypeStruct((rank, nf * cols), bf),
            jax.ShapeDtypeStruct((rank, rows), f32),
            jax.ShapeDtypeStruct((rank, cols), f32),
        ),
        in_specs=[pl.BlockSpec(memory_space=pl.ANY), pl.BlockSpec(memory_space=vmem)],
        out_specs=[pl.BlockSpec(memory_space=vmem)] * 3,
        scratch_shapes=[
            vmem((rows, nf * cols), bf),
            vmem((NC * NX, rows, ny * WIDE), bf),
            vmem((ITERS + 1, NC, NX, ny, rank, WIDE), bf),
            vmem((ITERS, nz, rank // 2, 2 * rows), f32),
            vmem((8, 128), f32),
            vmem((ITERS, NC, 8, 128), f32),
            vmem((ITERS, NX, 8, 128), f32),
            vmem((ITERS, ny, 8, 128), f32),
            vmem((ITERS, NC, NX, ny, rank, WIDE), f32),
            vmem((ITERS, NX, ny, rank, WIDE), f32),
            vmem((ITERS, NX - 1, ny, rank, WIDE), f32),
            vmem((ITERS, NX - 1, ny, rank, WIDE), f32),
            vmem((ITERS, ny - 1, rank, WIDE), f32),
            vmem((ITERS, nz, rank, WIDE), f32),
            dma,
            dma((ITERS + 1, n_ag)),
            dma((ITERS + 1, n_ag)),
            dma((ITERS, nz - 1)),
            dma((ITERS, nz - 1)),
            dma((ITERS, n_g)),
            dma((ITERS, n_g)),
            dma((ITERS, n_w)),
            dma((ITERS, n_w)),
        ],
        compiler_params=pltpu.CompilerParams(
            collective_id=0, has_side_effects=True, vmem_limit_bytes=48 * 1024 * 1024
        ),
    )(accumulated, q_start)
    approx = jnp.dot(basis_t.T.astype(bf), flat, preferred_element_type=f32)
    residual = (accumulated[0].astype(f32) - approx).astype(bf)[None]
    return residual, basis_t.T, q_factor


def solution(mesh):
    nz, nf = mesh.shape["rep"], mesh.shape["fsdp"]
    in_specs = (P("rep", "fsdp", None), P(None, "fsdp"))
    out_specs = (P("rep", "fsdp", None), P("fsdp", None), P(None, "fsdp"))
    return jax.shard_map(
        functools.partial(on_device, nz, nf),
        mesh=mesh,
        in_specs=in_specs,
        out_specs=out_specs,
        check_vma=False,
    )
```

time: 367 us -> 144 us (0.39)
  blocking collectives: 294 us -> 0 us
  Pallas kernels: 0 us -> 137 us
  other arithmetic: 21.9 us -> 0 us
  local copies, waits for them, and re-layouts: 18.8 us -> 3.43 us
  matrix products: 13.8 us -> 1.9 us
  waiting for transfers between devices: 9.09 us -> 0 us
  starting transfers between devices: 7.7 us -> 0 us
    all_to_all x10 -> x0, blocking collectives: 294 us -> none  [the longest x8 185 us: from_everyone(): lax.all_to_all(jnp.broadcast_to(x[None], (peers, *x.shape)), axis, 0, 0,...]
    pallas_call x0 -> x1, Pallas kernels: none -> 137 us  [on_device(): pl.pallas_call(functools.partial(kernel, nz, ny), out_shape=(jax.ShapeDty...]
    another operation x10 -> x0, other arithmetic: 13.4 us -> none  [the longest x6 7.2 us: orthonormal(): factor = jnp.linalg.cholesky(gram_matrix)]
    dot_general x7 -> x1, matrix products: 13.3 us -> 1.9 us  [on_device(): approx = jnp.dot(basis_t.T.astype(bf), flat, preferred_element_type=f32)]
    all_to_all x1 -> x0, waiting for transfers between devices: 9.09 us -> none  [from_everyone(): lax.all_to_all(jnp.broadcast_to(x[None], (peers, *x.shape)), axis, 0, 0,...]
    reshape x3 -> x0, local copies, waits for them, and re-layouts: 8.33 us -> none  [in_order(): blocks.reshape(*shape[:dim], shape[dim] * shape[dim + 1], *shape[dim + 2:])]
    all_to_all x1 -> x0, starting transfers between devices: 7.7 us -> none  [from_everyone(): lax.all_to_all(jnp.broadcast_to(x[None], (peers, *x.shape)), axis, 0, 0,...]
    all_to_all x4 -> x0, other arithmetic: 4.11 us -> none  [from_everyone(): lax.all_to_all(jnp.broadcast_to(x[None], (peers, *x.shape)), axis, 0, 0,...]
  transfers between devices with their start and end apart: 1 -> 0, of which waited for: 1 -> 0; matrix products, arithmetic and copies ran while one was open for 1% -> 0% of each run, Pallas kernels for 0% -> 0%
where the time goes in v1:
time: 144 us; the launch traced here: 143 us
  Pallas kernels  137 us (95%)
  local copies, waits for them, and re-layouts  3.43 us (2%)
  matrix products  1.9 us (1%)
    pallas_call x1, Pallas kernels, on_device(): pl.pallas_call(functools.partial(kernel, nz, ny), out_shape=(jax.ShapeDty...  137 us
    unnamed x6, local copies, waits for them, and re-layouts  3.43 us

profile of v1, /device:TPU:1, one launch (start us, length us, event | category | flops | bytes accessed | tf_op | source)
XLA Modules:
  0.0 143.3 jit_solution(7803081150614842178)
XLA Ops:
  0.6 0.0 copy-start
  0.6 1.5 %copy-done = bf16[1,64,14336]{2,1,0:T(8,128)(2,1)S(1)} copy-done((bf16[1,64,14336]{2,1,0:T(8,128)(2,1)S(1)}, bf16[1,64,14336]{2,1,0:T(8,128)(2,1)}, u32[]{:S(2)}) %copy-start) | copy-done | bytes 1835032
  2.1 0.0 copy-start.1
  2.1 0.7 copy-done.1
  2.8 137.4 %shard_map.49 = (bf16[32,14336]{1,0:T(8,128)(2,1)S(1)}, f32[32,64]{1,0:T(8,128)S(1)}, f32[32,224]{1,0:T(8,128)S(1)}) custom-call(bf16[1,64,14336]{2,1,0:T(8,128)(2,1)S(1)} %copy-done, bf16[32,224]{1,0:T(8,128)(2,1)S(1)} %copy-done.1), custom_call_target="tpu_custom_call" | custom-call | tf_op jit(solution)/shard_map/pallas_call | solution.py:311
  140.2 1.9 %fusion.1 = bf16[1,64,14336]{2,1,0:T(8,128)(2,1)} fusion(bf16[32,14336]{1,0:T(8,128)(2,1)S(1)} %get-tuple-element.7, bf16[1,64,14336]{2,1,0:T(8,128)(2,1)S(1)} %copy-done, f32[64,32]{0,1:T(8,128)S(1)} %bitcast.7), kind=kOutput, calls=%fused_computation.2 | convolution fusion | flops 61474816 | bytes 4595712 | tf_op jit(solution)/shard_map/dot_general | solution.py:349
  142.1 0.6 copy.7
  142.7 0.6 copy.8
Async XLA Ops:
  0.6 1.5 %copy-start = (bf16[1,64,14336]{2,1,0:T(8,128)(2,1)S(1)}, bf16[1,64,14336]{2,1,0:T(8,128)(2,1)}, u32[]{:S(2)}) copy-start(bf16[1,64,14336]{2,1,0:T(8,128)(2,1)} %a_hbm.1) | copy-start | bytes 5505028
  2.1 0.7 copy-start.1
